TPU v7x, 32 devices: a whole 2x2x4 slice. The times are simulated.
32 devices in a mesh: tm: 4 (over y, x), space: 8 (over z, core).
Axes of the slice: x: 2, y: 2, z: 4, core: 2. Of those that a mesh axis runs over, the one named last changes fastest.
Arguments:
- positions: float32 [4, 3, 3, 2048], P('tm', None, None, 'space'), may hold values from -4 to 4
- velocities: float32 [4, 3, 3, 2048], P('tm', None, None, 'space'), may hold values from -3 to 3
- masses: float32 [2048], P('space'), may hold values from 0.2 to 2
- initial_places: float32 [3, 2048], P(None, 'space'), may hold values from -4 to 4
- initial_speeds: float32 [3, 2048], P(None, 'space'), may hold values from -3 to 3
Outputs:
- node_places: float32 [4, 2, 3, 2048], P('tm', None, None, 'space')
- node_speeds: float32 [4, 2, 3, 2048], P('tm', None, None, 'space')
- end_force: float32 [4, 3, 2048], P('tm', None, 'space')
- start_places: float32 [4, 3, 2048], P('tm', None, 'space')
- start_speeds: float32 [4, 3, 2048], P('tm', None, 'space')
All inputs are finite; a program needn't handle non-finite values.
Results may differ from a plain program's by a relative error of at most 0.0003.
Values sent between devices are 32-bit elements; how exact they have to be, the bound alone decides.
A program may use at most 64 MiB of HBM per device.

v0:
```python
import functools
import jax
import jax.numpy as jnp
from jax import lax
from jax.experimental import pallas as pl
from jax.experimental.pallas import tpu as pltpu
from jax.sharding import PartitionSpec as P

soften = 0.01
slice_length = 0.25
lobatto_weights = ((5.0 / 24.0, 1.0 / 3.0, -1.0 / 24.0), (-1.0 / 24.0, 1.0 / 3.0, 5.0 / 24.0))
LANES = 128
MESH = pl.DeviceIdType.MESH
EARLY = 4


def round_up(value, step):
    return (value + step - 1) // step * step


def target_of(me, step, count):
    if count & (count - 1) == 0:
        peer, bit = 0, 1
        while bit < count:
            peer = peer + ((me // bit + step // bit) % 2) * bit
            bit *= 2
        return peer
    return (me + step) % count


def source_of(me, step, count):
    if count & (count - 1) == 0:
        return target_of(me, step, count)
    return (me + count - step) % count


def kernel(
    n, slices, body_count, chunk,
    pos, vel, mass, place0, speed0,
    places_out, speeds_out, force_out, start_out, start_speed_out,
    old, first, last, drift, speeds, own, load_sem, wide, total, force_rows,
    send_old, recv_old, send_first, recv_first, send_last, recv_last, send_drift, recv_drift,
):
    me = lax.axis_index("space")
    slot = lax.axis_index("tm")
    halves = mass.shape[0]
    block = halves * LANES
    rows = 3 * halves
    tile = old.shape[1] // 3

    barrier = pltpu.get_barrier_semaphore()
    for step in range(1, n):
        pl.semaphore_signal(barrier, inc=1, device_id={"space": target_of(me, step, n)}, device_id_type=MESH)
    for step in range(1, slices):
        pl.semaphore_signal(barrier, inc=1, device_id={"tm": (slot + step) % slices}, device_id_type=MESH)

    def lanes_of(half):
        return pl.ds(half * LANES, LANES)

    loads = [
        pltpu.make_async_copy(mass.at[:, 0, :], old.at[me, pl.ds(rows, halves), :], load_sem.at[0]),
        pltpu.make_async_copy(place0, own.at[0], load_sem.at[1]),
        pltpu.make_async_copy(speed0, own.at[1], load_sem.at[2]),
    ]
    for node in range(3):
        span = pl.ds(node * rows, rows)
        loads.append(pltpu.make_async_copy(pos.at[span, 0, :], old.at[me, pl.ds(node * tile, rows), :], load_sem.at[3 + node]))
        loads.append(pltpu.make_async_copy(vel.at[span, 0, :], speeds.at[node, pl.ds(0, rows), :], load_sem.at[6 + node]))
    for load in loads:
        load.start()
    for load in loads:
        load.wait()

    speed = [speeds[node, pl.ds(0, rows), :] for node in range(3)]
    x0 = old[me, pl.ds(0, rows), :]
    half_step = 0.5 * slice_length

    def moved(weights):
        return slice_length * (weights[0] * speed[0] + weights[1] * speed[1] + weights[2] * speed[2])

    x1 = x0 + half_step * (speed[0] - speed[0]) + moved(lobatto_weights[0])
    first[me, pl.ds(0, rows), :] = x1

    def widen(node, ref, offset):
        for comp in range(3):
            for half in range(halves):
                line = ref[me, pl.ds(offset + comp * halves + half, 1), :]
                wide[node, comp, lanes_of(half), :] = jnp.broadcast_to(line, (LANES, LANES)).T

    def copy(ref, send, recv, step):
        return pltpu.make_async_remote_copy(
            src_ref=ref.at[me], dst_ref=ref.at[me], send_sem=send.at[step], recv_sem=recv.at[step],
            device_id={"space": target_of(me, step, n)}, device_id_type=MESH,
        )

    def arrival(ref, send, recv, step):
        whose = source_of(me, step, n)
        pltpu.make_async_remote_copy(
            src_ref=ref.at[whose], dst_ref=ref.at[whose], send_sem=send.at[step], recv_sem=recv.at[step],
            device_id={"space": target_of(me, step, n)}, device_id_type=MESH,
        ).wait_recv()
        return whose

    def pairs(whose, parts, fresh):
        def one_chunk(index, carry):
            span = pl.ds(pl.multiple_of(index * chunk, chunk), chunk)
            for node, ref, offset in parts:
                here = [wide[node, comp, span, :] for comp in range(3)]
                sums = [None] * 3 if fresh else [total[node, comp, span, :] for comp in range(3)]
                for half in range(halves):
                    gap = [ref[whose, pl.ds(offset + comp * halves + half, 1), :] - here[comp] for comp in range(3)]
                    weight = old[whose, pl.ds(rows + half, 1), :]
                    squared = gap[0] * gap[0] + gap[1] * gap[1] + gap[2] * gap[2]
                    inverse = lax.rsqrt(squared + soften)
                    pull = (inverse * inverse) * (inverse * weight)
                    sums = [pull * gap[comp] if sums[comp] is None else sums[comp] + pull * gap[comp] for comp in range(3)]
                for comp in range(3):
                    total[node, comp, span, :] = sums[comp]
            return carry

        lax.fori_loop(0, block // chunk, one_chunk, 0)

    ones = jnp.ones((8, 2 * LANES), jnp.bfloat16)

    def finish(node):
        sums = total[node].reshape(3 * block, LANES)
        high = sums.astype(jnp.bfloat16)
        low = (sums - high.astype(jnp.float32)).astype(jnp.bfloat16)
        both = jnp.concatenate([high, low], axis=1)
        line = lax.dot_general(ones, both, (((1,), (1,)), ((), ())), preferred_element_type=jnp.float32)
        for row in range(rows):
            force_rows[node, pl.ds(row, 1), :] = line[0:1, row * LANES:(row + 1) * LANES]
        return force_rows[node, pl.ds(0, rows), :] / body_count

    old_parts = [(node, old, node * tile) for node in range(3)]
    first_part = [(3, first, 0)]
    last_part = [(4, last, 0)]

    for node in range(3):
        widen(node, old, node * tile)
    pl.semaphore_wait(barrier, n - 1 + slices - 1)
    for step in range(1, n):
        copy(old, send_old, recv_old, step).start()
    for step in range(1, n):
        copy(first, send_first, recv_first, step).start()
    pairs(me, old_parts, True)
    widen(3, first, 0)
    pairs(me, first_part, True)

    def with_first(step, carry):
        whose = arrival(old, send_old, recv_old, step)
        pairs(whose, old_parts, False)
        return carry

    lax.fori_loop(1, n, with_first, 0)

    a_old = [finish(node) for node in range(3)]

    def kicked(weights):
        return slice_length * (weights[0] * a_old[0] + weights[1] * a_old[1] + weights[2] * a_old[2])

    v0, a0 = speed[0], a_old[0]
    v1 = v0 + half_step * (a0 - a_old[0]) + kicked(lobatto_weights[0])
    x2 = x1 + half_step * (v1 - speed[1]) + moved(lobatto_weights[1])
    last[me, pl.ds(0, rows), :] = x2
    for step in range(1, n):
        copy(last, send_last, recv_last, step).start()

    def only_first(step, carry):
        whose = arrival(first, send_first, recv_first, step)
        pairs(whose, first_part, False)
        return carry

    lax.fori_loop(1, n, only_first, 0)
    a1 = finish(3)
    v2 = v1 + half_step * (a1 - a_old[1]) + kicked(lobatto_weights[1])
    drift_rows = drift.shape[1] // 2
    drift[slot, pl.ds(0, rows), :] = x2 - (x0 + slice_length * v0)
    drift[slot, pl.ds(drift_rows, rows), :] = v2 - v0

    def drift_copy(step, whose, to):
        return pltpu.make_async_remote_copy(
            src_ref=drift.at[whose], dst_ref=drift.at[whose], send_sem=send_drift.at[step], recv_sem=recv_drift.at[step],
            device_id={"tm": to}, device_id_type=MESH,
        )

    for step in range(1, slices):
        drift_copy(step, slot, (slot + step) % slices).start()

    widen(4, last, 0)
    pairs(me, last_part, True)

    def put(ref, value):
        for row in range(rows):
            ref[row] = value[row:row + 1, :]

    def put_pair(ref, value1, value2):
        for comp in range(3):
            for half in range(halves):
                row = comp * halves + half
                ref[comp, half, 0:1, :] = value1[row:row + 1, :]
                ref[comp, half, 1:2, :] = value2[row:row + 1, :]

    put_pair(places_out, x1, x2)
    put_pair(speeds_out, v1, v2)

    def only_last(step, carry):
        whose = arrival(last, send_last, recv_last, step)
        pairs(whose, last_part, False)
        return carry

    lax.fori_loop(1, n, only_last, 0)
    a2 = finish(4)
    put(force_out, a2)

    def in_rows(value):
        return jnp.concatenate(
            [value[comp:comp + 1, half * LANES:(half + 1) * LANES] for comp in range(3) for half in range(halves)], axis=0
        )

    start_speed = in_rows(own[1])
    start_place = in_rows(own[0]) + slot.astype(jnp.float32) * slice_length * start_speed
    for step in range(1, slices):
        whose = (slot + slices - step) % slices
        drift_copy(step, whose, whose).wait_recv()
        moved_place = drift[whose, pl.ds(0, rows), :]
        moved_speed = drift[whose, pl.ds(drift_rows, rows), :]
        ahead = (slot - 1 - whose).astype(jnp.float32) * slice_length
        counts = whose < slot
        start_place = start_place + jnp.where(counts, moved_place + ahead * moved_speed, 0.0)
        start_speed = start_speed + jnp.where(counts, moved_speed, 0.0)
    put(start_out, start_place)
    put(start_speed_out, start_speed)

    for step in range(1, n):
        copy(old, send_old, recv_old, step).wait_send()
        copy(first, send_first, recv_first, step).wait_send()
        copy(last, send_last, recv_last, step).wait_send()
    for step in range(1, slices):
        drift_copy(step, slot, (slot + step) % slices).wait_send()


def write_out(*refs):
    copies = [pltpu.make_async_copy(refs[i], refs[5 + i], refs[10].at[i]) for i in range(5)]
    for copy in copies:
        copy.start()
    for copy in copies:
        copy.wait()


def solution(mesh):
    n, slices = mesh.shape["space"], mesh.shape["tm"]

    def body(positions, velocities, masses, initial_places, initial_speeds):
        block = positions.shape[3]
        halves = block // LANES
        tile = round_up(4 * halves, 8)
        part = round_up(3 * halves, 8)
        f32 = jnp.float32
        vmem = pl.BlockSpec(memory_space=pltpu.VMEM)
        dma = pltpu.SemaphoreType.DMA
        rows = 3 * halves
        shapes = [(3, halves, 2, LANES)] * 2 + [(rows, 1, LANES)] * 3
        anywhere = pl.BlockSpec(memory_space=pl.ANY)
        outs = pl.pallas_call(
            functools.partial(kernel, n, slices, float(block * n), 64),
            out_shape=tuple(pltpu.VMEM(shape, f32) for shape in shapes),
            in_specs=[anywhere] * 5,
            out_specs=(vmem,) * 5,
            scratch_shapes=[
                pltpu.VMEM((n, 3 * tile, LANES), f32),
                pltpu.VMEM((n, part, LANES), f32),
                pltpu.VMEM((n, part, LANES), f32),
                pltpu.VMEM((slices, 2 * part, LANES), f32),
                pltpu.VMEM((3, part, LANES), f32),
                pltpu.VMEM((2, 3, block), f32),
                dma((9,)),
                pltpu.VMEM((5, 3, block, LANES), f32),
                pltpu.VMEM((5, 3, block, LANES), f32),
                pltpu.VMEM((5, part, LANES), f32),
                dma((n,)), dma((n,)), dma((n,)), dma((n,)), dma((n,)), dma((n,)),
                dma((slices,)), dma((slices,)),
            ],
            compiler_params=pltpu.CompilerParams(collective_id=0, has_side_effects=True),
        )(
            positions.reshape(3 * rows, 1, LANES),
            velocities.reshape(3 * rows, 1, LANES),
            masses.reshape(halves, 1, LANES),
            initial_places,
            initial_speeds,
        )
        outs = pl.pallas_call(
            write_out,
            out_shape=tuple(jax.ShapeDtypeStruct(shape, f32) for shape in shapes),
            in_specs=[vmem] * 5,
            out_specs=(anywhere,) * 5,
            scratch_shapes=[dma((5,))],
        )(*(pltpu.with_memory_space_constraint(part, pltpu.VMEM) for part in outs))
        paired = [part.transpose(2, 0, 1, 3).reshape(1, 2, 3, block) for part in outs[:2]]
        return (*paired, *(part.reshape(1, 3, block) for part in outs[2:]))

    return jax.shard_map(
        body,
        mesh=mesh,
        in_specs=(
            P("tm", None, None, "space"),
            P("tm", None, None, "space"),
            P("space"),
            P(None, "space"),
            P(None, "space"),
        ),
        out_specs=(
            P("tm", None, None, "space"),
            P("tm", None, None, "space"),
            P("tm", None, "space"),
            P("tm", None, "space"),
            P("tm", None, "space"),
        ),
        check_vma=False,
    )
```

profile of v0, /device:TPU:0, one launch (start us, length us, event | category | flops | bytes accessed | tf_op | source)
XLA Modules:
  0.0 19.0 jit_solution(256098703042080664)
XLA Ops:
  0.6 17.8 %shard_map.92 = (f32[3,2,2,128]{3,2,1,0:T(2,128)S(1)}, f32[3,2,2,128]{3,2,1,0:T(2,128)S(1)}, f32[6,1,128]{2,1,0:T(1,128)S(1)}, f32[6,1,128]{2,1,0:T(1,128)S(1)}, f32[6,1,128]{2,1,0:T(1,128)S(1)}) custom-call(f32[18,1,128]{2,1,0:T(1,128)} %bitcast.12, f32[18,1,128]{2,1,0:T(1,128)} %bitcast.13, f32[2,1,128]{2,1,0:T(1,128)} %bitcast.14, f32[3,256]{1,0:T(4,128)} %place0.1, ...), custom_call_target="tpu_custom_call" | custom-call | tf_op jit(solution)/shard_map/pallas_call | solution.py:265
  18.4 0.7 %shard_map.93 = (f32[3,2,2,128]{3,2,1,0:T(2,128)}, f32[3,2,2,128]{3,2,1,0:T(2,128)}, f32[6,1,128]{2,1,0:T(1,128)}, f32[6,1,128]{2,1,0:T(1,128)}, f32[6,1,128]{2,1,0:T(1,128)}) custom-call(f32[3,2,2,128]{3,2,1,0:T(2,128)S(1)} %get-tuple-element.15.refs_0_, f32[3,2,2,128]{3,2,1,0:T(2,128)S(1)} %get-tuple-element.16.refs_1_, ...), custom_call_target="tpu_custom_call" | custom-call | tf_op jit(solution)/shard_map/pallas_call | solution.py:292
where the time goes:
time: 19.2 us; the launch traced here: 19 us
  Pallas kernels  18.4 us (96%)
  between operations  0.64 us (3%)
    pallas_call x1, Pallas kernels, body(): pl.pallas_call(functools.partial(kernel, n, slices, float(block * n), 64)...  17.8 us
    pallas_call x1, Pallas kernels, body(): pl.pallas_call(write_out, out_shape=tuple((jax.ShapeDtypeStruct(shape, f3...  0.65 us

commit v1 on v0

v1 whole, which is shorter than its diff:
```python
import functools
import jax
import jax.numpy as jnp
from jax import lax
from jax.experimental import pallas as pl
from jax.experimental.pallas import tpu as pltpu
from jax.sharding import PartitionSpec as P

soften = 0.01
slice_length = 0.25
lobatto_weights = ((5.0 / 24.0, 1.0 / 3.0, -1.0 / 24.0), (-1.0 / 24.0, 1.0 / 3.0, 5.0 / 24.0))
LANES = 128
MESH = pl.DeviceIdType.MESH


def round_up(value, step):
    return (value + step - 1) // step * step


def target_of(me, step, count):
    if count & (count - 1) == 0:
        peer, bit = 0, 1
        while bit < count:
            peer = peer + ((me // bit + step // bit) % 2) * bit
            bit *= 2
        return peer
    return (me + step) % count


def source_of(me, step, count):
    if count & (count - 1) == 0:
        return target_of(me, step, count)
    return (me + count - step) % count


def kernel(
    n, slices, body_count, chunk,
    pos, vel, mass, place0, speed0,
    places_out, speeds_out, force_out, start_out, start_speed_out,
    old, first, last, drift, speeds, own, load_sem, wide, total,
    send_old, recv_old, send_first, recv_first, send_last, recv_last, send_drift, recv_drift, ready, go,
):
    me = lax.axis_index("space")
    slot = lax.axis_index("tm")
    halves = mass.shape[0]
    block = halves * LANES
    rows = 3 * halves
    weigh = rows
    base = (0, rows + halves, 2 * rows + halves)
    used = 3 * rows + halves
    f32 = jnp.float32

    barrier = pltpu.get_barrier_semaphore()
    for step in range(1, n):
        pl.semaphore_signal(barrier, inc=1, device_id={"space": target_of(me, step, n)}, device_id_type=MESH)

    @pl.when(me == 0)
    def _():
        for step in range(1, slices):
            pl.semaphore_signal(barrier, inc=1, device_id={"tm": (slot + step) % slices}, device_id_type=MESH)

    loads = [
        pltpu.make_async_copy(mass.at[:, 0, :], old.at[me, pl.ds(weigh, halves), :], load_sem.at[0]),
        pltpu.make_async_copy(place0, own.at[0], load_sem.at[1]),
        pltpu.make_async_copy(speed0, own.at[1], load_sem.at[2]),
    ]
    for node in range(3):
        span = pl.ds(node * rows, rows)
        loads.append(pltpu.make_async_copy(pos.at[span, 0, :], old.at[me, pl.ds(base[node], rows), :], load_sem.at[3 + node]))
        loads.append(pltpu.make_async_copy(vel.at[span, 0, :], speeds.at[node, pl.ds(0, rows), :], load_sem.at[6 + node]))
    for load in loads:
        load.start()
    for load in loads:
        load.wait()

    def copy(ref, count, send, recv, step):
        span = pl.ds(0, count)
        return pltpu.make_async_remote_copy(
            src_ref=ref.at[me, span, :], dst_ref=ref.at[me, span, :], send_sem=send.at[step], recv_sem=recv.at[step],
            device_id={"space": target_of(me, step, n)}, device_id_type=MESH,
        )

    def arrival(ref, count, send, recv, step):
        whose = source_of(me, step, n)
        span = pl.ds(0, count)
        pltpu.make_async_remote_copy(
            src_ref=ref.at[whose, span, :], dst_ref=ref.at[whose, span, :], send_sem=send.at[step], recv_sem=recv.at[step],
            device_id={"space": target_of(me, step, n)}, device_id_type=MESH,
        ).wait_recv()
        return whose

    pl.semaphore_wait(barrier, n - 1 + jnp.where(me == 0, slices - 1, 0))
    for step in range(1, n):
        copy(old, used, send_old, recv_old, step).start()

    speed = [speeds[node, pl.ds(0, rows), :] for node in range(3)]
    x0 = old[me, pl.ds(0, rows), :]
    half_step = 0.5 * slice_length

    def moved(weights):
        return slice_length * (weights[0] * speed[0] + weights[1] * speed[1] + weights[2] * speed[2])

    x1 = x0 + half_step * (speed[0] - speed[0]) + moved(lobatto_weights[0])
    first[me, pl.ds(0, rows), :] = x1
    for step in range(1, n):
        copy(first, rows, send_first, recv_first, step).start()

    @pl.when(me == 0)
    def _():
        for step in range(1, slices):
            pl.semaphore_signal(ready, inc=1, device_id={"tm": (slot + step) % slices}, device_id_type=MESH)

    def lanes_of(half):
        return pl.ds(half * LANES, LANES)

    def widen(node, ref, offset):
        for comp in range(3):
            for half in range(halves):
                line = ref[me, pl.ds(offset + comp * halves + half, 1), :]
                wide[node, comp, lanes_of(half), :] = jnp.broadcast_to(line, (LANES, LANES)).T

    def pairs(whose, parts, fresh):
        def one_chunk(index, carry):
            span = pl.ds(pl.multiple_of(index * chunk, chunk), chunk)
            for node, ref, offset in parts:
                here = [wide[node, comp, span, :] for comp in range(3)]
                sums = [None] * 3 if fresh else [total[node, comp, span, :] for comp in range(3)]
                for half in range(halves):
                    gap = [ref[whose, pl.ds(offset + comp * halves + half, 1), :] - here[comp] for comp in range(3)]
                    weight = old[whose, pl.ds(weigh + half, 1), :]
                    squared = gap[0] * gap[0] + gap[1] * gap[1] + gap[2] * gap[2]
                    inverse = lax.rsqrt(squared + soften)
                    pull = (inverse * inverse) * (inverse * weight)
                    sums = [pull * gap[comp] if sums[comp] is None else sums[comp] + pull * gap[comp] for comp in range(3)]
                for comp in range(3):
                    total[node, comp, span, :] = sums[comp]
            return carry

        lax.fori_loop(0, block // chunk, one_chunk, 0)

    ones = jnp.ones((8, 2 * LANES), jnp.bfloat16)

    def folded(comps):
        parts = []
        for comp in range(3):
            sums = comps[comp]
            high = sums.astype(jnp.bfloat16)
            low = (sums - high.astype(f32)).astype(jnp.bfloat16)
            both = jnp.concatenate([high, low], axis=1)
            line = lax.dot_general(ones, both, (((1,), (1,)), ((), ())), preferred_element_type=f32)
            parts.extend(line[0:1, half * LANES:(half + 1) * LANES] for half in range(halves))
        return jnp.concatenate(parts, axis=0) / body_count

    def added(node):
        return [total[node, comp] for comp in range(3)]

    old_parts = [(node, old, base[node]) for node in range(3)]

    def use_old(whose, fresh):
        pairs(whose, old_parts, fresh)

    def use_new(node, ref, whose, fresh):
        if fresh:
            widen(node, ref, 0)
        pairs(whose, [(node, ref, 0)], fresh)

    for node in range(3):
        widen(node, old, base[node])
    use_old(me, True)

    def with_old(step, carry):
        use_old(arrival(old, used, send_old, recv_old, step), False)
        return carry

    lax.fori_loop(1, n, with_old, 0)

    def kicked(weights, drop):
        parts = [weights[node] * slice_length for node in range(3)]
        parts[1] = parts[1] - drop
        return folded([parts[0] * total[0, comp] + parts[1] * total[1, comp] + parts[2] * total[2, comp] for comp in range(3)])

    v0 = speed[0]
    v1 = v0 + kicked(lobatto_weights[0], 0.0)
    x2 = x1 + half_step * (v1 - speed[1]) + moved(lobatto_weights[1])
    last[me, pl.ds(0, rows), :] = x2
    for step in range(1, n):
        copy(last, rows, send_last, recv_last, step).start()

    @pl.when(me == 0)
    def _():
        pl.semaphore_wait(ready, slices - 1)
        for step in range(1, n):
            pl.semaphore_signal(go, inc=1, device_id={"space": step}, device_id_type=MESH)

    kick = kicked(lobatto_weights[1], half_step)
    use_new(3, first, me, True)

    def only_first(step, carry):
        use_new(3, first, arrival(first, rows, send_first, recv_first, step), False)
        return carry

    lax.fori_loop(1, n, only_first, 0)
    a1 = folded(added(3))
    v2 = v1 + half_step * a1 + kick
    drift_rows = drift.shape[1] // 2
    drift[slot, pl.ds(0, rows), :] = x2 - (x0 + slice_length * v0)
    drift[slot, pl.ds(drift_rows, rows), :] = v2 - v0

    def drift_copy(step, whose, to):
        return pltpu.make_async_remote_copy(
            src_ref=drift.at[whose], dst_ref=drift.at[whose], send_sem=send_drift.at[step], recv_sem=recv_drift.at[step],
            device_id={"tm": to}, device_id_type=MESH,
        )

    @pl.when(me != 0)
    def _():
        pl.semaphore_wait(go, 1)

    for step in range(1, slices):
        @pl.when(slot + step < slices)
        def _():
            drift_copy(step, slot, slot + step).start()

    use_new(4, last, me, True)

    def put(ref, value):
        for row in range(rows):
            ref[row] = value[row:row + 1, :]

    def put_pair(ref, value1, value2):
        for comp in range(3):
            for half in range(halves):
                row = comp * halves + half
                ref[comp, half, 0:1, :] = value1[row:row + 1, :]
                ref[comp, half, 1:2, :] = value2[row:row + 1, :]

    put_pair(places_out, x1, x2)
    put_pair(speeds_out, v1, v2)

    def in_rows(value):
        return jnp.concatenate(
            [value[comp:comp + 1, half * LANES:(half + 1) * LANES] for comp in range(3) for half in range(halves)], axis=0
        )

    start_speed = in_rows(own[1])
    put(start_speed_out, start_speed)
    put(start_out, in_rows(own[0]) + slot.astype(f32) * slice_length * start_speed)

    def only_last(step, carry):
        use_new(4, last, arrival(last, rows, send_last, recv_last, step), False)
        return carry

    lax.fori_loop(1, n, only_last, 0)
    put(force_out, folded(added(4)))

    for step in range(1, slices):
        @pl.when(slot >= step)
        def _():
            whose = slot - step
            drift_copy(step, whose, whose).wait_recv()
            moved_place = drift[whose, pl.ds(0, rows), :]
            moved_speed = drift[whose, pl.ds(drift_rows, rows), :]
            ahead = moved_place + ((step - 1) * slice_length) * moved_speed
            for row in range(rows):
                start_out[row] = start_out[row] + ahead[row:row + 1, :]
                start_speed_out[row] = start_speed_out[row] + moved_speed[row:row + 1, :]

    for step in range(1, n):
        copy(old, used, send_old, recv_old, step).wait_send()
        copy(first, rows, send_first, recv_first, step).wait_send()
        copy(last, rows, send_last, recv_last, step).wait_send()
    for step in range(1, slices):
        @pl.when(slot + step < slices)
        def _():
            drift_copy(step, slot, slot + step).wait_send()


def write_out(*refs):
    copies = [pltpu.make_async_copy(refs[i], refs[5 + i], refs[10].at[i]) for i in range(5)]
    for copy in copies:
        copy.start()
    for copy in copies:
        copy.wait()


def solution(mesh):
    n, slices = mesh.shape["space"], mesh.shape["tm"]

    def body(positions, velocities, masses, initial_places, initial_speeds):
        block = positions.shape[3]
        halves = block // LANES
        stack = round_up(10 * halves, 8)
        part = round_up(3 * halves, 8)
        f32 = jnp.float32
        vmem = pl.BlockSpec(memory_space=pltpu.VMEM)
        dma = pltpu.SemaphoreType.DMA
        rows = 3 * halves
        shapes = [(3, halves, 2, LANES)] * 2 + [(rows, 1, LANES)] * 3
        anywhere = pl.BlockSpec(memory_space=pl.ANY)
        outs = pl.pallas_call(
            functools.partial(kernel, n, slices, float(block * n), 64),
            out_shape=tuple(pltpu.VMEM(shape, f32) for shape in shapes),
            in_specs=[anywhere] * 5,
            out_specs=(vmem,) * 5,
            scratch_shapes=[
                pltpu.VMEM((n, stack, LANES), f32),
                pltpu.VMEM((n, part, LANES), f32),
                pltpu.VMEM((n, part, LANES), f32),
                pltpu.VMEM((slices, 2 * part, LANES), f32),
                pltpu.VMEM((3, part, LANES), f32),
                pltpu.VMEM((2, 3, block), f32),
                dma((9,)),
                pltpu.VMEM((5, 3, block, LANES), f32),
                pltpu.VMEM((5, 3, block, LANES), f32),
                dma((n,)), dma((n,)), dma((n,)), dma((n,)), dma((n,)), dma((n,)),
                dma((slices,)), dma((slices,)),
                pltpu.SemaphoreType.REGULAR, pltpu.SemaphoreType.REGULAR,
            ],
            compiler_params=pltpu.CompilerParams(collective_id=0, has_side_effects=True),
        )(
            positions.reshape(3 * rows, 1, LANES),
            velocities.reshape(3 * rows, 1, LANES),
            masses.reshape(halves, 1, LANES),
            initial_places,
            initial_speeds,
        )
        outs = pl.pallas_call(
            write_out,
            out_shape=tuple(jax.ShapeDtypeStruct(shape, f32) for shape in shapes),
            in_specs=[vmem] * 5,
            out_specs=(anywhere,) * 5,
            scratch_shapes=[dma((5,))],
        )(*(pltpu.with_memory_space_constraint(part, pltpu.VMEM) for part in outs))
        paired = [part.transpose(2, 0, 1, 3).reshape(1, 2, 3, block) for part in outs[:2]]
        return (*paired, *(part.reshape(1, 3, block) for part in outs[2:]))

    return jax.shard_map(
        body,
        mesh=mesh,
        in_specs=(
            P("tm", None, None, "space"),
            P("tm", None, None, "space"),
            P("space"),
            P(None, "space"),
            P(None, "space"),
        ),
        out_specs=(
            P("tm", None, None, "space"),
            P("tm", None, None, "space"),
            P("tm", None, "space"),
            P("tm", None, "space"),
            P("tm", None, "space"),
        ),
        check_vma=False,
    )
```

time: 19.2 us -> 17.6 us (0.917)
  Pallas kernels: 18.4 us -> 16.8 us
    pallas_call x1, Pallas kernels: 17.8 us -> 16.1 us  [body(): pl.pallas_call(functools.partial(kernel, n, slices, float(block * n), 64)...]
where the time goes in v1:
time: 17.6 us; the launch traced here: 17.4 us
  Pallas kernels  16.8 us (95%)
  between operations  0.64 us (4%)
    pallas_call x1, Pallas kernels, body(): pl.pallas_call(functools.partial(kernel, n, slices, float(block * n), 64)...  16.1 us
    pallas_call x1, Pallas kernels, body(): pl.pallas_call(write_out, out_shape=tuple((jax.ShapeDtypeStruct(shape, f3...  0.65 us

profile of v1, /device:TPU:0, one launch (start us, length us, event | category | flops | bytes accessed | tf_op | source)
XLA Modules:
  0.0 17.4 jit_solution(2399955645456837505)
XLA Ops:
  0.6 16.1 %shard_map.92 = (f32[3,2,2,128]{3,2,1,0:T(2,128)S(1)}, f32[3,2,2,128]{3,2,1,0:T(2,128)S(1)}, f32[6,1,128]{2,1,0:T(1,128)S(1)}, f32[6,1,128]{2,1,0:T(1,128)S(1)}, f32[6,1,128]{2,1,0:T(1,128)S(1)}) custom-call(f32[18,1,128]{2,1,0:T(1,128)} %bitcast.12, f32[18,1,128]{2,1,0:T(1,128)} %bitcast.13, f32[2,1,128]{2,1,0:T(1,128)} %bitcast.14, f32[3,256]{1,0:T(4,128)} %place0.1, ...), custom_call_target="tpu_custom_call" | custom-call | tf_op jit(solution)/shard_map/pallas_call | solution.py:300
  16.8 0.7 %shard_map.93 = (f32[3,2,2,128]{3,2,1,0:T(2,128)}, f32[3,2,2,128]{3,2,1,0:T(2,128)}, f32[6,1,128]{2,1,0:T(1,128)}, f32[6,1,128]{2,1,0:T(1,128)}, f32[6,1,128]{2,1,0:T(1,128)}) custom-call(f32[3,2,2,128]{3,2,1,0:T(2,128)S(1)} %get-tuple-element.15.refs_0_, f32[3,2,2,128]{3,2,1,0:T(2,128)S(1)} %get-tuple-element.16.refs_1_, ...), custom_call_target="tpu_custom_call" | custom-call | tf_op jit(solution)/shard_map/pallas_call | solution.py:327

commit v2 on v1

--- a/solution.py
+++ b/solution.py
@@ -38,7 +38,7 @@
     pos, vel, mass, place0, speed0,
     places_out, speeds_out, force_out, start_out, start_speed_out,
     old, first, last, drift, speeds, own, load_sem, wide, total,
-    send_old, recv_old, send_first, recv_first, send_last, recv_last, send_drift, recv_drift, ready, go,
+    send_old, recv_old, send_first, recv_first, send_last, recv_last, send_drift, recv_drift, ready, go, arrive,
 ):
     me = lax.axis_index("space")
     slot = lax.axis_index("tm")
@@ -50,11 +50,14 @@
     used = 3 * rows + halves
     f32 = jnp.float32
 
+    leader = 0
     barrier = pltpu.get_barrier_semaphore()
-    for step in range(1, n):
-        pl.semaphore_signal(barrier, inc=1, device_id={"space": target_of(me, step, n)}, device_id_type=MESH)
-
-    @pl.when(me == 0)
+    for other in range(1, n):
+        @pl.when(other > me)
+        def _():
+            pl.semaphore_signal(barrier, inc=1, device_id={"space": other}, device_id_type=MESH)
+
+    @pl.when(me == leader)
     def _():
         for step in range(1, slices):
             pl.semaphore_signal(barrier, inc=1, device_id={"tm": (slot + step) % slices}, device_id_type=MESH)
@@ -70,28 +73,61 @@
         loads.append(pltpu.make_async_copy(vel.at[span, 0, :], speeds.at[node, pl.ds(0, rows), :], load_sem.at[6 + node]))
     for load in loads:
         load.start()
+
+    @pl.when(me > 0)
+    def _():
+        pl.semaphore_wait(barrier, me)
+
+    for other in range(n - 1):
+        @pl.when(other < me)
+        def _():
+            pl.semaphore_signal(arrive.at[me], inc=1, device_id={"space": other}, device_id_type=MESH)
+
     for load in loads:
         load.wait()
 
-    def copy(ref, count, send, recv, step):
+    chips = n // 2
+    chip, core = me // 2, me % 2
+
+    def copy(ref, count, send, recv, to):
         span = pl.ds(0, count)
         return pltpu.make_async_remote_copy(
-            src_ref=ref.at[me, span, :], dst_ref=ref.at[me, span, :], send_sem=send.at[step], recv_sem=recv.at[step],
-            device_id={"space": target_of(me, step, n)}, device_id_type=MESH,
+            src_ref=ref.at[me, span, :], dst_ref=ref.at[me, span, :], send_sem=send.at[to], recv_sem=recv.at[me],
+            device_id={"space": to}, device_id_type=MESH,
         )
 
+    def whose_at(step):
+        far = (step - 2) // 2
+        above = chip + 1 + far
+        side = (step - 2) % 2
+        flip = core + side - 2 * core * side
+        other = 2 * jnp.where(above < chips, above, chips - 2 - far) + flip
+        return jnp.where(step == 1, me + 1 - 2 * core, other)
+
     def arrival(ref, count, send, recv, step):
-        whose = source_of(me, step, n)
+        whose = whose_at(step)
         span = pl.ds(0, count)
         pltpu.make_async_remote_copy(
-            src_ref=ref.at[whose, span, :], dst_ref=ref.at[whose, span, :], send_sem=send.at[step], recv_sem=recv.at[step],
-            device_id={"space": target_of(me, step, n)}, device_id_type=MESH,
+            src_ref=ref.at[whose, span, :], dst_ref=ref.at[whose, span, :], send_sem=send.at[whose], recv_sem=recv.at[whose],
+            device_id={"space": whose}, device_id_type=MESH,
         ).wait_recv()
         return whose
 
-    pl.semaphore_wait(barrier, n - 1 + jnp.where(me == 0, slices - 1, 0))
-    for step in range(1, n):
-        copy(old, used, send_old, recv_old, step).start()
+    def up(index):
+        return index + jnp.where(index < me, 0, 1)
+
+    def seq(index):
+        if index == 0:
+            return me + 1 - 2 * core
+        far, side = (index - 1) // 2, (index - 1) % 2
+        above = chip + 1 + far
+        flip = core + side - 2 * core * side
+        return 2 * jnp.where(above < chips, above, chips - 2 - far) + flip
+
+    for other in range(n - 1):
+        @pl.when(other < me)
+        def _():
+            copy(old, used, send_old, recv_old, other).start()
 
     speed = [speeds[node, pl.ds(0, rows), :] for node in range(3)]
     x0 = old[me, pl.ds(0, rows), :]
@@ -102,13 +138,10 @@
 
     x1 = x0 + half_step * (speed[0] - speed[0]) + moved(lobatto_weights[0])
     first[me, pl.ds(0, rows), :] = x1
-    for step in range(1, n):
-        copy(first, rows, send_first, recv_first, step).start()
-
-    @pl.when(me == 0)
-    def _():
-        for step in range(1, slices):
-            pl.semaphore_signal(ready, inc=1, device_id={"tm": (slot + step) % slices}, device_id_type=MESH)
+
+    def meet(other):
+        pl.semaphore_wait(arrive.at[other], 1)
+        copy(old, used, send_old, recv_old, other).start()
 
     def lanes_of(half):
         return pl.ds(half * LANES, LANES)
@@ -166,7 +199,27 @@
 
     for node in range(3):
         widen(node, old, base[node])
+    near = 2 * chip + 4
+    for other in range(1, n):
+        @pl.when((other > me) & (other < near))
+        def _():
+            meet(other)
+
     use_old(me, True)
+    for other in range(1, n):
+        @pl.when((other > me) & (other >= near))
+        def _():
+            meet(other)
+
+    for index in range(n - 1):
+        copy(first, rows, send_first, recv_first, seq(index)).start()
+
+    @pl.when(me == leader)
+    def _():
+        pl.semaphore_wait(barrier, slices - 1)
+        for step in range(1, slices):
+            pl.semaphore_signal(ready, inc=1, device_id={"tm": (slot + step) % slices}, device_id_type=MESH)
+
 
     def with_old(step, carry):
         use_old(arrival(old, used, send_old, recv_old, step), False)
@@ -183,14 +236,15 @@
     v1 = v0 + kicked(lobatto_weights[0], 0.0)
     x2 = x1 + half_step * (v1 - speed[1]) + moved(lobatto_weights[1])
     last[me, pl.ds(0, rows), :] = x2
-    for step in range(1, n):
-        copy(last, rows, send_last, recv_last, step).start()
-
-    @pl.when(me == 0)
+    for index in range(n - 1):
+        copy(last, rows, send_last, recv_last, up(index)).start()
+
+    @pl.when(me == leader)
     def _():
         pl.semaphore_wait(ready, slices - 1)
-        for step in range(1, n):
-            pl.semaphore_signal(go, inc=1, device_id={"space": step}, device_id_type=MESH)
+        for other in range(n):
+            if other != leader:
+                pl.semaphore_signal(go, inc=1, device_id={"space": other}, device_id_type=MESH)
 
     kick = kicked(lobatto_weights[1], half_step)
     use_new(3, first, me, True)
@@ -212,7 +266,7 @@
             device_id={"tm": to}, device_id_type=MESH,
         )
 
-    @pl.when(me != 0)
+    @pl.when(me != leader)
     def _():
         pl.semaphore_wait(go, 1)
 
@@ -266,9 +320,9 @@
                 start_speed_out[row] = start_speed_out[row] + moved_speed[row:row + 1, :]
 
     for step in range(1, n):
-        copy(old, used, send_old, recv_old, step).wait_send()
-        copy(first, rows, send_first, recv_first, step).wait_send()
-        copy(last, rows, send_last, recv_last, step).wait_send()
+        copy(old, used, send_old, recv_old, target_of(me, step, n)).wait_send()
+        copy(first, rows, send_first, recv_first, target_of(me, step, n)).wait_send()
+        copy(last, rows, send_last, recv_last, target_of(me, step, n)).wait_send()
     for step in range(1, slices):
         @pl.when(slot + step < slices)
         def _():
@@ -298,7 +352,7 @@
         shapes = [(3, halves, 2, LANES)] * 2 + [(rows, 1, LANES)] * 3
         anywhere = pl.BlockSpec(memory_space=pl.ANY)
         outs = pl.pallas_call(
-            functools.partial(kernel, n, slices, float(block * n), 64),
+            functools.partial(kernel, n, slices, float(block * n), 128),
             out_shape=tuple(pltpu.VMEM(shape, f32) for shape in shapes),
             in_specs=[anywhere] * 5,
             out_specs=(vmem,) * 5,
@@ -314,7 +368,7 @@
                 pltpu.VMEM((5, 3, block, LANES), f32),
                 dma((n,)), dma((n,)), dma((n,)), dma((n,)), dma((n,)), dma((n,)),
                 dma((slices,)), dma((slices,)),
-                pltpu.SemaphoreType.REGULAR, pltpu.SemaphoreType.REGULAR,
+                pltpu.SemaphoreType.REGULAR, pltpu.SemaphoreType.REGULAR, pltpu.SemaphoreType.REGULAR((n,)),
             ],
             compiler_params=pltpu.CompilerParams(collective_id=0, has_side_effects=True),
         )(

time: 17.6 us -> 17.2 us (0.977)
  Pallas kernels: 16.8 us -> 16.4 us
    pallas_call x1, Pallas kernels: 16.1 us -> 15.8 us  [body(): pl.pallas_call(functools.partial(kernel, n, slices, float(block * n), 128...]
where the time goes in v2:
time: 17.2 us; the launch traced here: 17.1 us
  Pallas kernels  16.4 us (95%)
  between operations  0.64 us (4%)
    pallas_call x1, Pallas kernels, body(): pl.pallas_call(functools.partial(kernel, n, slices, float(block * n), 128...  15.8 us
    pallas_call x1, Pallas kernels, body(): pl.pallas_call(write_out, out_shape=tuple((jax.ShapeDtypeStruct(shape, f3...  0.65 us

profile of v2, /device:TPU:0, one launch (start us, length us, event | category | flops | bytes accessed | tf_op | source)
XLA Modules:
  0.0 17.1 jit_solution(16609701233435424901)
XLA Ops:
  0.6 15.8 %shard_map.92 = (f32[3,2,2,128]{3,2,1,0:T(2,128)S(1)}, f32[3,2,2,128]{3,2,1,0:T(2,128)S(1)}, f32[6,1,128]{2,1,0:T(1,128)S(1)}, f32[6,1,128]{2,1,0:T(1,128)S(1)}, f32[6,1,128]{2,1,0:T(1,128)S(1)}) custom-call(f32[18,1,128]{2,1,0:T(1,128)} %bitcast.12, f32[18,1,128]{2,1,0:T(1,128)} %bitcast.13, f32[2,1,128]{2,1,0:T(1,128)} %bitcast.14, f32[3,256]{1,0:T(4,128)} %place0.1, ...), custom_call_target="tpu_custom_call" | custom-call | tf_op jit(solution)/shard_map/pallas_call | solution.py:354
  16.4 0.7 %shard_map.93 = (f32[3,2,2,128]{3,2,1,0:T(2,128)}, f32[3,2,2,128]{3,2,1,0:T(2,128)}, f32[6,1,128]{2,1,0:T(1,128)}, f32[6,1,128]{2,1,0:T(1,128)}, f32[6,1,128]{2,1,0:T(1,128)}) custom-call(f32[3,2,2,128]{3,2,1,0:T(2,128)S(1)} %get-tuple-element.15.refs_0_, f32[3,2,2,128]{3,2,1,0:T(2,128)S(1)} %get-tuple-element.16.refs_1_, ...), custom_call_target="tpu_custom_call" | custom-call | tf_op jit(solution)/shard_map/pallas_call | solution.py:381

commit v3 on v2

--- a/solution.py
+++ b/solution.py
@@ -50,18 +50,6 @@
     used = 3 * rows + halves
     f32 = jnp.float32
 
-    leader = 0
-    barrier = pltpu.get_barrier_semaphore()
-    for other in range(1, n):
-        @pl.when(other > me)
-        def _():
-            pl.semaphore_signal(barrier, inc=1, device_id={"space": other}, device_id_type=MESH)
-
-    @pl.when(me == leader)
-    def _():
-        for step in range(1, slices):
-            pl.semaphore_signal(barrier, inc=1, device_id={"tm": (slot + step) % slices}, device_id_type=MESH)
-
     loads = [
         pltpu.make_async_copy(mass.at[:, 0, :], old.at[me, pl.ds(weigh, halves), :], load_sem.at[0]),
         pltpu.make_async_copy(place0, own.at[0], load_sem.at[1]),
@@ -74,6 +62,18 @@
     for load in loads:
         load.start()
 
+    leader = 0
+    barrier = pltpu.get_barrier_semaphore()
+    for other in range(1, n):
+        @pl.when(other > me)
+        def _():
+            pl.semaphore_signal(barrier, inc=1, device_id={"space": other}, device_id_type=MESH)
+
+    @pl.when(me == leader)
+    def _():
+        for step in range(1, slices):
+            pl.semaphore_signal(barrier, inc=1, device_id={"tm": (slot + step) % slices}, device_id_type=MESH)
+
     @pl.when(me > 0)
     def _():
         pl.semaphore_wait(barrier, me)
@@ -98,10 +98,9 @@
 
     def whose_at(step):
         far = (step - 2) // 2
-        above = chip + 1 + far
         side = (step - 2) % 2
         flip = core + side - 2 * core * side
-        other = 2 * jnp.where(above < chips, above, chips - 2 - far) + flip
+        other = 2 * jnp.where(far < chip, chip - 1 - far, far + 1) + flip
         return jnp.where(step == 1, me + 1 - 2 * core, other)
 
     def arrival(ref, count, send, recv, step):
@@ -176,12 +175,9 @@
     def folded(comps):
         parts = []
         for comp in range(3):
-            sums = comps[comp]
-            high = sums.astype(jnp.bfloat16)
-            low = (sums - high.astype(f32)).astype(jnp.bfloat16)
-            both = jnp.concatenate([high, low], axis=1)
-            line = lax.dot_general(ones, both, (((1,), (1,)), ((), ())), preferred_element_type=f32)
-            parts.extend(line[0:1, half * LANES:(half + 1) * LANES] for half in range(halves))
+            for half in range(halves):
+                turned = comps[comp][half * LANES:(half + 1) * LANES, :].T
+                parts.append(jnp.sum(turned, axis=0, keepdims=True))
         return jnp.concatenate(parts, axis=0) / body_count
 
     def added(node):
@@ -299,6 +295,13 @@
     start_speed = in_rows(own[1])
     put(start_speed_out, start_speed)
     put(start_out, in_rows(own[0]) + slot.astype(f32) * slice_length * start_speed)
+
+    for step in range(1, n):
+        copy(old, used, send_old, recv_old, target_of(me, step, n)).wait_send()
+        copy(first, rows, send_first, recv_first, target_of(me, step, n)).wait_send()
+
+    for step in range(1, n):
+        copy(last, rows, send_last, recv_last, target_of(me, step, n)).wait_send()
 
     def only_last(step, carry):
         use_new(4, last, arrival(last, rows, send_last, recv_last, step), False)
@@ -319,10 +322,6 @@
                 start_out[row] = start_out[row] + ahead[row:row + 1, :]
                 start_speed_out[row] = start_speed_out[row] + moved_speed[row:row + 1, :]
 
-    for step in range(1, n):
-        copy(old, used, send_old, recv_old, target_of(me, step, n)).wait_send()
-        copy(first, rows, send_first, recv_first, target_of(me, step, n)).wait_send()
-        copy(last, rows, send_last, recv_last, target_of(me, step, n)).wait_send()
     for step in range(1, slices):
         @pl.when(slot + step < slices)
         def _():
@@ -352,7 +351,7 @@
         shapes = [(3, halves, 2, LANES)] * 2 + [(rows, 1, LANES)] * 3
         anywhere = pl.BlockSpec(memory_space=pl.ANY)
         outs = pl.pallas_call(
-            functools.partial(kernel, n, slices, float(block * n), 128),
+            functools.partial(kernel, n, slices, float(block * n), 64),
             out_shape=tuple(pltpu.VMEM(shape, f32) for shape in shapes),
             in_specs=[anywhere] * 5,
             out_specs=(vmem,) * 5,

time: 17.2 us -> 16.9 us (0.983)
  Pallas kernels: 16.4 us -> 16.1 us
    pallas_call x1, Pallas kernels: 15.8 us -> 15.5 us  [body(): pl.pallas_call(functools.partial(kernel, n, slices, float(block * n), 64)...]
where the time goes in v3:
time: 16.9 us; the launch traced here: 16.8 us
  Pallas kernels  16.1 us (95%)
  between operations  0.64 us (4%)
    pallas_call x1, Pallas kernels, body(): pl.pallas_call(functools.partial(kernel, n, slices, float(block * n), 64)...  15.5 us
    pallas_call x1, Pallas kernels, body(): pl.pallas_call(write_out, out_shape=tuple((jax.ShapeDtypeStruct(shape, f3...  0.65 us

profile of v3, /device:TPU:0, one launch (start us, length us, event | category | flops | bytes accessed | tf_op | source)
XLA Modules:
  0.0 16.8 jit_solution(1015540291202600053)
XLA Ops:
  0.6 15.5 %shard_map.92 = (f32[3,2,2,128]{3,2,1,0:T(2,128)S(1)}, f32[3,2,2,128]{3,2,1,0:T(2,128)S(1)}, f32[6,1,128]{2,1,0:T(1,128)S(1)}, f32[6,1,128]{2,1,0:T(1,128)S(1)}, f32[6,1,128]{2,1,0:T(1,128)S(1)}) custom-call(f32[18,1,128]{2,1,0:T(1,128)} %bitcast.12, f32[18,1,128]{2,1,0:T(1,128)} %bitcast.13, f32[2,1,128]{2,1,0:T(1,128)} %bitcast.14, f32[3,256]{1,0:T(4,128)} %place0.1, ...), custom_call_target="tpu_custom_call" | custom-call | tf_op jit(solution)/shard_map/pallas_call | solution.py:353
  16.1 0.7 %shard_map.93 = (f32[3,2,2,128]{3,2,1,0:T(2,128)}, f32[3,2,2,128]{3,2,1,0:T(2,128)}, f32[6,1,128]{2,1,0:T(1,128)}, f32[6,1,128]{2,1,0:T(1,128)}, f32[6,1,128]{2,1,0:T(1,128)}) custom-call(f32[3,2,2,128]{3,2,1,0:T(2,128)S(1)} %get-tuple-element.15.refs_0_, f32[3,2,2,128]{3,2,1,0:T(2,128)S(1)} %get-tuple-element.16.refs_1_, ...), custom_call_target="tpu_custom_call" | custom-call | tf_op jit(solution)/shard_map/pallas_call | solution.py:380

commit v4 on v3

--- a/solution.py
+++ b/solution.py
@@ -123,7 +123,7 @@
         flip = core + side - 2 * core * side
         return 2 * jnp.where(above < chips, above, chips - 2 - far) + flip
 
-    for other in range(n - 1):
+    for other in reversed(range(n - 1)):
         @pl.when(other < me)
         def _():
             copy(old, used, send_old, recv_old, other).start()
@@ -153,19 +153,20 @@
 
     def pairs(whose, parts, fresh):
         def one_chunk(index, carry):
-            span = pl.ds(pl.multiple_of(index * chunk, chunk), chunk)
             for node, ref, offset in parts:
-                here = [wide[node, comp, span, :] for comp in range(3)]
-                sums = [None] * 3 if fresh else [total[node, comp, span, :] for comp in range(3)]
-                for half in range(halves):
-                    gap = [ref[whose, pl.ds(offset + comp * halves + half, 1), :] - here[comp] for comp in range(3)]
-                    weight = old[whose, pl.ds(weigh + half, 1), :]
-                    squared = gap[0] * gap[0] + gap[1] * gap[1] + gap[2] * gap[2]
-                    inverse = lax.rsqrt(squared + soften)
-                    pull = (inverse * inverse) * (inverse * weight)
-                    sums = [pull * gap[comp] if sums[comp] is None else sums[comp] + pull * gap[comp] for comp in range(3)]
-                for comp in range(3):
-                    total[node, comp, span, :] = sums[comp]
+                for part in range(chunk // 16):
+                    span = pl.ds(pl.multiple_of(index * chunk, chunk) + part * 16, 16)
+                    here = [wide[node, comp, span, :] for comp in range(3)]
+                    sums = [None] * 3 if fresh else [total[node, comp, span, :] for comp in range(3)]
+                    for half in range(halves):
+                        gap = [ref[whose, pl.ds(offset + comp * halves + half, 1), :] - here[comp] for comp in range(3)]
+                        weight = old[whose, pl.ds(weigh + half, 1), :]
+                        squared = gap[0] * gap[0] + gap[1] * gap[1] + gap[2] * gap[2]
+                        inverse = lax.rsqrt(squared + soften)
+                        pull = (inverse * inverse) * (inverse * weight)
+                        sums = [pull * gap[comp] if sums[comp] is None else sums[comp] + pull * gap[comp] for comp in range(3)]
+                    for comp in range(3):
+                        total[node, comp, span, :] = sums[comp]
             return carry
 
         lax.fori_loop(0, block // chunk, one_chunk, 0)
@@ -351,7 +352,7 @@
         shapes = [(3, halves, 2, LANES)] * 2 + [(rows, 1, LANES)] * 3
         anywhere = pl.BlockSpec(memory_space=pl.ANY)
         outs = pl.pallas_call(
-            functools.partial(kernel, n, slices, float(block * n), 64),
+            functools.partial(kernel, n, slices, float(block * n), block),
             out_shape=tuple(pltpu.VMEM(shape, f32) for shape in shapes),
             in_specs=[anywhere] * 5,
             out_specs=(vmem,) * 5,

time: 16.9 us -> 16.8 us (level)
  no operation moved by 1% of the time
where the time goes in v4:
time: 16.8 us; the launch traced here: 16.6 us
  Pallas kernels  16 us (95%)
  between operations  0.64 us (4%)
    pallas_call x1, Pallas kernels, body(): pl.pallas_call(functools.partial(kernel, n, slices, float(block * n), blo...  15.3 us
    pallas_call x1, Pallas kernels, body(): pl.pallas_call(write_out, out_shape=tuple((jax.ShapeDtypeStruct(shape, f3...  0.65 us

profile of v4, /device:TPU:0, one launch (start us, length us, event | category | flops | bytes accessed | tf_op | source)
XLA Modules:
  0.0 16.6 jit_solution(17265097746767780901)
XLA Ops:
  0.6 15.3 %shard_map.92 = (f32[3,2,2,128]{3,2,1,0:T(2,128)S(1)}, f32[3,2,2,128]{3,2,1,0:T(2,128)S(1)}, f32[6,1,128]{2,1,0:T(1,128)S(1)}, f32[6,1,128]{2,1,0:T(1,128)S(1)}, f32[6,1,128]{2,1,0:T(1,128)S(1)}) custom-call(f32[18,1,128]{2,1,0:T(1,128)} %bitcast.12, f32[18,1,128]{2,1,0:T(1,128)} %bitcast.13, f32[2,1,128]{2,1,0:T(1,128)} %bitcast.14, f32[3,256]{1,0:T(4,128)} %place0.1, ...), custom_call_target="tpu_custom_call" | custom-call | tf_op jit(solution)/shard_map/pallas_call | solution.py:354
  15.9 0.7 %shard_map.93 = (f32[3,2,2,128]{3,2,1,0:T(2,128)}, f32[3,2,2,128]{3,2,1,0:T(2,128)}, f32[6,1,128]{2,1,0:T(1,128)}, f32[6,1,128]{2,1,0:T(1,128)}, f32[6,1,128]{2,1,0:T(1,128)}) custom-call(f32[3,2,2,128]{3,2,1,0:T(2,128)S(1)} %get-tuple-element.15.refs_0_, f32[3,2,2,128]{3,2,1,0:T(2,128)S(1)} %get-tuple-element.16.refs_1_, ...), custom_call_target="tpu_custom_call" | custom-call | tf_op jit(solution)/shard_map/pallas_call | solution.py:381

commit v5 on v4

--- a/solution.py
+++ b/solution.py
@@ -78,7 +78,7 @@
     def _():
         pl.semaphore_wait(barrier, me)
 
-    for other in range(n - 1):
+    for other in reversed(range(n - 1)):
         @pl.when(other < me)
         def _():
             pl.semaphore_signal(arrive.at[me], inc=1, device_id={"space": other}, device_id_type=MESH)
@@ -179,7 +179,7 @@
             for half in range(halves):
                 turned = comps[comp][half * LANES:(half + 1) * LANES, :].T
                 parts.append(jnp.sum(turned, axis=0, keepdims=True))
-        return jnp.concatenate(parts, axis=0) / body_count
+        return jnp.concatenate(parts, axis=0) * (1.0 / body_count)
 
     def added(node):
         return [total[node, comp] for comp in range(3)]

time: 16.8 us -> 16.7 us (level)
  no operation moved by 1% of the time
where the time goes in v5:
time: 16.7 us; the launch traced here: 16.6 us
  Pallas kernels  16 us (96%)
  between operations  0.64 us (4%)
    pallas_call x1, Pallas kernels, body(): pl.pallas_call(functools.partial(kernel, n, slices, float(block * n), blo...  15.3 us
    pallas_call x1, Pallas kernels, body(): pl.pallas_call(write_out, out_shape=tuple((jax.ShapeDtypeStruct(shape, f3...  0.65 us

profile of v5, /device:TPU:0, one launch (start us, length us, event | category | flops | bytes accessed | tf_op | source)
XLA Modules:
  0.0 16.6 jit_solution(3263640315097998047)
XLA Ops:
  0.6 15.3 %shard_map.92 = (f32[3,2,2,128]{3,2,1,0:T(2,128)S(1)}, f32[3,2,2,128]{3,2,1,0:T(2,128)S(1)}, f32[6,1,128]{2,1,0:T(1,128)S(1)}, f32[6,1,128]{2,1,0:T(1,128)S(1)}, f32[6,1,128]{2,1,0:T(1,128)S(1)}) custom-call(f32[18,1,128]{2,1,0:T(1,128)} %bitcast.12, f32[18,1,128]{2,1,0:T(1,128)} %bitcast.13, f32[2,1,128]{2,1,0:T(1,128)} %bitcast.14, f32[3,256]{1,0:T(4,128)} %place0.1, ...), custom_call_target="tpu_custom_call" | custom-call | tf_op jit(solution)/shard_map/pallas_call | solution.py:354
  15.9 0.7 %shard_map.93 = (f32[3,2,2,128]{3,2,1,0:T(2,128)}, f32[3,2,2,128]{3,2,1,0:T(2,128)}, f32[6,1,128]{2,1,0:T(1,128)}, f32[6,1,128]{2,1,0:T(1,128)}, f32[6,1,128]{2,1,0:T(1,128)}) custom-call(f32[3,2,2,128]{3,2,1,0:T(2,128)S(1)} %get-tuple-element.15.refs_0_, f32[3,2,2,128]{3,2,1,0:T(2,128)S(1)} %get-tuple-element.16.refs_1_, ...), custom_call_target="tpu_custom_call" | custom-call | tf_op jit(solution)/shard_map/pallas_call | solution.py:381
